TPU v7x, 8 devices: a whole 2x2x1 slice. The times are simulated.
8 devices in a mesh: col: 4 (over z, y, x), row: 2 (over core).
Axes of the slice: x: 2, y: 2, z: 1, core: 2. Of those that a mesh axis runs over, the one named last changes fastest.
Arguments:
- adjacency: bfloat16 [16384, 16384], P('row', 'col')
- x_init: float32 [16384, 128], P(('col', 'row'))
- teleport: float32 [16384, 128], P(('col', 'row'))
- dangling: int32 [16384], P(('col', 'row'))
- damping: float32 [32], replicated
Outputs:
- output 1: float32 [16384, 128], P(('col', 'row'))
- output 2: float32 [32, 128], replicated
All inputs are finite; a program needn't handle non-finite values.
Results may differ from a plain program's by a relative error of at most 0.001.
Values are sent between devices in bfloat16 or wider.
A program may use at most 1 GiB of HBM per device.

v0:
```python
import jax
import jax.numpy as jnp
from jax import lax
from jax.sharding import PartitionSpec as P


def layout_pairs(n_row, n_col):
    return [(col_idx * n_row + row_idx, row_idx * n_col + col_idx) for row_idx in range(n_row) for col_idx in range(n_col)]


def solution(mesh):
    n_row = mesh.shape["row"]
    n_col = mesh.shape["col"]
    both_axes = ("col", "row")
    pairs = layout_pairs(n_row, n_col)

    def sweeps(adj_tile, x_piece, tele_piece, dang_piece, damping):
        n_vert = adj_tile.shape[0] * n_row
        dang_mask = dang_piece[:, None] > 0
        x_cur = x_piece
        resid_rows = []
        for step in range(damping.shape[0]):
            d_step = damping[step]
            dang_mass = lax.psum(jnp.sum(jnp.where(dang_mask, x_cur, 0.0), axis=0), both_axes)
            x_source = lax.all_gather(x_cur.astype(jnp.bfloat16), "row", axis=0, tiled=True)
            partial_prod = jnp.dot(adj_tile, x_source, preferred_element_type=jnp.float32)
            folded = lax.psum_scatter(partial_prod, "col", scatter_dimension=0, tiled=True)
            moved = lax.ppermute(folded, both_axes, pairs)
            x_next = d_step * moved + (d_step * dang_mass / n_vert + (1.0 - d_step)) * tele_piece
            resid_rows.append(lax.psum(jnp.sum(jnp.abs(x_next - x_cur), axis=0), both_axes) / n_vert)
            x_cur = x_next
        return x_cur, jnp.stack(resid_rows)

    vec_spec = P(both_axes, None)
    return jax.shard_map(sweeps, mesh=mesh, in_specs=(P("row", "col"), vec_spec, vec_spec, P(both_axes), P()), out_specs=(vec_spec, P()), check_vma=False)
```

profile of v0, /device:TPU:0, one launch (start us, length us, event | category | flops | bytes accessed | tf_op | source)
XLA Modules:
  0.0 4311.3 jit_solution(15134471727801190035)
XLA Ops:
  49.1 48.1 %reduce-scatter.33.cloned.1.call-done = f32[2048,128]{1,0:T(8,128)} async-done(((f32[8192,128]{1,0:T(8,128)}), f32[2048,128]{1,0:T(8,128)}) %reduce-scatter.33.cloned.1.call-update) | async-done | bytes 1048592 | tf_op jit(solution)/shard_map/reduce_scatter | solution.py:27
  182.0 48.1 %reduce-scatter.35.cloned.1.call-done = f32[2048,128]{1,0:T(8,128)} async-done(((f32[8192,128]{1,0:T(8,128)}), f32[2048,128]{1,0:T(8,128)}) %reduce-scatter.35.cloned.1.call-update) | async-done | bytes 1048592 | tf_op jit(solution)/shard_map/reduce_scatter | solution.py:27
  314.9 48.1 %reduce-scatter.37.cloned.1.call-done = f32[2048,128]{1,0:T(8,128)} async-done(((f32[8192,128]{1,0:T(8,128)}), f32[2048,128]{1,0:T(8,128)}) %reduce-scatter.37.cloned.1.call-update) | async-done | bytes 1048592 | tf_op jit(solution)/shard_map/reduce_scatter | solution.py:27
  447.8 48.1 %reduce-scatter.39.cloned.1.call-done = f32[2048,128]{1,0:T(8,128)} async-done(((f32[8192,128]{1,0:T(8,128)}), f32[2048,128]{1,0:T(8,128)}) %reduce-scatter.39.cloned.1.call-update) | async-done | bytes 1048592 | tf_op jit(solution)/shard_map/reduce_scatter | solution.py:27
  498.3 42.2 psum.451
  580.4 48.1 %reduce-scatter.41.cloned.1.call-done = f32[2048,128]{1,0:T(8,128)} async-done(((f32[8192,128]{1,0:T(8,128)}), f32[2048,128]{1,0:T(8,128)}) %reduce-scatter.41.cloned.1.call-update) | async-done | bytes 1048592 | tf_op jit(solution)/shard_map/reduce_scatter | solution.py:27
  713.4 48.1 %reduce-scatter.43.cloned.1.call-done = f32[2048,128]{1,0:T(8,128)} async-done(((f32[8192,128]{1,0:T(8,128)}), f32[2048,128]{1,0:T(8,128)}) %reduce-scatter.43.cloned.1.call-update) | async-done | bytes 1048592 | tf_op jit(solution)/shard_map/reduce_scatter | solution.py:27
  846.3 48.1 %reduce-scatter.45.cloned.1.call-done = f32[2048,128]{1,0:T(8,128)} async-done(((f32[8192,128]{1,0:T(8,128)}), f32[2048,128]{1,0:T(8,128)}) %reduce-scatter.45.cloned.1.call-update) | async-done | bytes 1048592 | tf_op jit(solution)/shard_map/reduce_scatter | solution.py:27
  896.9 42.2 psum.454
  979.0 48.1 %reduce-scatter.47.cloned.1.call-done = f32[2048,128]{1,0:T(8,128)} async-done(((f32[8192,128]{1,0:T(8,128)}), f32[2048,128]{1,0:T(8,128)}) %reduce-scatter.47.cloned.1.call-update) | async-done | bytes 1048592 | tf_op jit(solution)/shard_map/reduce_scatter | solution.py:27
  1029.6 42.1 psum.455
  1111.8 48.1 %reduce-scatter.49.cloned.1.call-done = f32[2048,128]{1,0:T(8,128)} async-done(((f32[8192,128]{1,0:T(8,128)}), f32[2048,128]{1,0:T(8,128)}) %reduce-scatter.49.cloned.1.call-update) | async-done | bytes 1048592 | tf_op jit(solution)/shard_map/reduce_scatter | solution.py:27
  1244.7 48.1 %reduce-scatter.51.cloned.1.call-done = f32[2048,128]{1,0:T(8,128)} async-done(((f32[8192,128]{1,0:T(8,128)}), f32[2048,128]{1,0:T(8,128)}) %reduce-scatter.51.cloned.1.call-update) | async-done | bytes 1048592 | tf_op jit(solution)/shard_map/reduce_scatter | solution.py:27
  1295.3 42.1 psum.457
  1377.5 48.1 %reduce-scatter.53.cloned.1.call-done = f32[2048,128]{1,0:T(8,128)} async-done(((f32[8192,128]{1,0:T(8,128)}), f32[2048,128]{1,0:T(8,128)}) %reduce-scatter.53.cloned.1.call-update) | async-done | bytes 1048592 | tf_op jit(solution)/shard_map/reduce_scatter | solution.py:27
  1428.1 42.1 psum.458
  1510.3 48.1 %reduce-scatter.55.cloned.1.call-done = f32[2048,128]{1,0:T(8,128)} async-done(((f32[8192,128]{1,0:T(8,128)}), f32[2048,128]{1,0:T(8,128)}) %reduce-scatter.55.cloned.1.call-update) | async-done | bytes 1048592 | tf_op jit(solution)/shard_map/reduce_scatter | solution.py:27
  1560.9 42.2 psum.459
  1643.0 48.1 %reduce-scatter.57.cloned.1.call-done = f32[2048,128]{1,0:T(8,128)} async-done(((f32[8192,128]{1,0:T(8,128)}), f32[2048,128]{1,0:T(8,128)}) %reduce-scatter.57.cloned.1.call-update) | async-done | bytes 1048592 | tf_op jit(solution)/shard_map/reduce_scatter | solution.py:27
  1777.0 48.1 %reduce-scatter.59.cloned.1.call-done = f32[2048,128]{1,0:T(8,128)} async-done(((f32[8192,128]{1,0:T(8,128)}), f32[2048,128]{1,0:T(8,128)}) %reduce-scatter.59.cloned.1.call-update) | async-done | bytes 1048592 | tf_op jit(solution)/shard_map/reduce_scatter | solution.py:27
  1915.9 48.1 %reduce-scatter.61.cloned.1.call-done = f32[2048,128]{1,0:T(8,128)} async-done(((f32[8192,128]{1,0:T(8,128)}), f32[2048,128]{1,0:T(8,128)}) %reduce-scatter.61.cloned.1.call-update) | async-done | bytes 1048592 | tf_op jit(solution)/shard_map/reduce_scatter | solution.py:27
  1966.4 42.2 psum.462
  2048.6 48.1 %reduce-scatter.63.cloned.1.call-done = f32[2048,128]{1,0:T(8,128)} async-done(((f32[8192,128]{1,0:T(8,128)}), f32[2048,128]{1,0:T(8,128)}) %reduce-scatter.63.cloned.1.call-update) | async-done | bytes 1048592 | tf_op jit(solution)/shard_map/reduce_scatter | solution.py:27
  2181.5 48.1 %reduce-scatter.65.cloned.1.call-done = f32[2048,128]{1,0:T(8,128)} async-done(((f32[8192,128]{1,0:T(8,128)}), f32[2048,128]{1,0:T(8,128)}) %reduce-scatter.65.cloned.1.call-update) | async-done | bytes 1048592 | tf_op jit(solution)/shard_map/reduce_scatter | solution.py:27
  2314.5 48.1 %reduce-scatter.67.cloned.1.call-done = f32[2048,128]{1,0:T(8,128)} async-done(((f32[8192,128]{1,0:T(8,128)}), f32[2048,128]{1,0:T(8,128)}) %reduce-scatter.67.cloned.1.call-update) | async-done | bytes 1048592 | tf_op jit(solution)/shard_map/reduce_scatter | solution.py:27
  2365.0 42.2 psum.465
  2447.3 48.1 %reduce-scatter.69.cloned.1.call-done = f32[2048,128]{1,0:T(8,128)} async-done(((f32[8192,128]{1,0:T(8,128)}), f32[2048,128]{1,0:T(8,128)}) %reduce-scatter.69.cloned.1.call-update) | async-done | bytes 1048592 | tf_op jit(solution)/shard_map/reduce_scatter | solution.py:27
  2580.2 48.1 %reduce-scatter.71.cloned.1.call-done = f32[2048,128]{1,0:T(8,128)} async-done(((f32[8192,128]{1,0:T(8,128)}), f32[2048,128]{1,0:T(8,128)}) %reduce-scatter.71.cloned.1.call-update) | async-done | bytes 1048592 | tf_op jit(solution)/shard_map/reduce_scatter | solution.py:27
  2630.8 42.1 psum.467
  2713.0 48.1 %reduce-scatter.73.cloned.1.call-done = f32[2048,128]{1,0:T(8,128)} async-done(((f32[8192,128]{1,0:T(8,128)}), f32[2048,128]{1,0:T(8,128)}) %reduce-scatter.73.cloned.1.call-update) | async-done | bytes 1048592 | tf_op jit(solution)/shard_map/reduce_scatter | solution.py:27
  2763.6 42.1 psum.468
  2845.8 48.1 %reduce-scatter.75.cloned.1.call-done = f32[2048,128]{1,0:T(8,128)} async-done(((f32[8192,128]{1,0:T(8,128)}), f32[2048,128]{1,0:T(8,128)}) %reduce-scatter.75.cloned.1.call-update) | async-done | bytes 1048592 | tf_op jit(solution)/shard_map/reduce_scatter | solution.py:27
  2896.4 42.2 psum.469
  2978.6 48.1 %reduce-scatter.77.cloned.1.call-done = f32[2048,128]{1,0:T(8,128)} async-done(((f32[8192,128]{1,0:T(8,128)}), f32[2048,128]{1,0:T(8,128)}) %reduce-scatter.77.cloned.1.call-update) | async-done | bytes 1048592 | tf_op jit(solution)/shard_map/reduce_scatter | solution.py:27
  3029.3 42.1 psum.470
  3111.5 48.1 %reduce-scatter.79.cloned.1.call-done = f32[2048,128]{1,0:T(8,128)} async-done(((f32[8192,128]{1,0:T(8,128)}), f32[2048,128]{1,0:T(8,128)}) %reduce-scatter.79.cloned.1.call-update) | async-done | bytes 1048592 | tf_op jit(solution)/shard_map/reduce_scatter | solution.py:27
  3162.0 42.2 psum.471
  3244.2 48.1 %reduce-scatter.81.cloned.1.call-done = f32[2048,128]{1,0:T(8,128)} async-done(((f32[8192,128]{1,0:T(8,128)}), f32[2048,128]{1,0:T(8,128)}) %reduce-scatter.81.cloned.1.call-update) | async-done | bytes 1048592 | tf_op jit(solution)/shard_map/reduce_scatter | solution.py:27
  3377.1 48.1 %reduce-scatter.83.cloned.1.call-done = f32[2048,128]{1,0:T(8,128)} async-done(((f32[8192,128]{1,0:T(8,128)}), f32[2048,128]{1,0:T(8,128)}) %reduce-scatter.83.cloned.1.call-update) | async-done | bytes 1048592 | tf_op jit(solution)/shard_map/reduce_scatter | solution.py:27
  3510.1 48.1 %reduce-scatter.85.cloned.1.call-done = f32[2048,128]{1,0:T(8,128)} async-done(((f32[8192,128]{1,0:T(8,128)}), f32[2048,128]{1,0:T(8,128)}) %reduce-scatter.85.cloned.1.call-update) | async-done | bytes 1048592 | tf_op jit(solution)/shard_map/reduce_scatter | solution.py:27
  3560.6 42.2 psum.474
  3642.8 48.1 %reduce-scatter.87.cloned.1.call-done = f32[2048,128]{1,0:T(8,128)} async-done(((f32[8192,128]{1,0:T(8,128)}), f32[2048,128]{1,0:T(8,128)}) %reduce-scatter.87.cloned.1.call-update) | async-done | bytes 1048592 | tf_op jit(solution)/shard_map/reduce_scatter | solution.py:27
  3693.5 42.1 psum.475
  3775.7 48.1 %reduce-scatter.89.cloned.1.call-done = f32[2048,128]{1,0:T(8,128)} async-done(((f32[8192,128]{1,0:T(8,128)}), f32[2048,128]{1,0:T(8,128)}) %reduce-scatter.89.cloned.1.call-update) | async-done | bytes 1048592 | tf_op jit(solution)/shard_map/reduce_scatter | solution.py:27
  3826.3 42.2 psum.476
  3908.4 48.1 %reduce-scatter.91.cloned.1.call-done = f32[2048,128]{1,0:T(8,128)} async-done(((f32[8192,128]{1,0:T(8,128)}), f32[2048,128]{1,0:T(8,128)}) %reduce-scatter.91.cloned.1.call-update) | async-done | bytes 1048592 | tf_op jit(solution)/shard_map/reduce_scatter | solution.py:27
  4041.4 48.1 %reduce-scatter.93.cloned.1.call-done = f32[2048,128]{1,0:T(8,128)} async-done(((f32[8192,128]{1,0:T(8,128)}), f32[2048,128]{1,0:T(8,128)}) %reduce-scatter.93.cloned.1.call-update) | async-done | bytes 1048592 | tf_op jit(solution)/shard_map/reduce_scatter | solution.py:27
  4175.3 48.2 %reduce-scatter.95.cloned.1.call-done = f32[2048,128]{1,0:T(8,128)} async-done(((f32[8192,128]{1,0:T(8,128)}), f32[2048,128]{1,0:T(8,128)}) %reduce-scatter.95.cloned.1.call-update) | async-done | bytes 1048592 | tf_op jit(solution)/shard_map/reduce_scatter | solution.py:27
  (491 shorter events, 2059.5 us)
Async XLA Ops:
  10.8 86.5 %reduce-scatter.33.cloned.1.call-start = ((), (), s32[]{:S(2)}) async-start(), calls=%async_computation.33 | async-start | bytes 5242880 | tf_op jit(solution)/shard_map/reduce_scatter | solution.py:27
  49.1 103.7 %all-gather.35.cloned.1.call-start = ((), (), s32[]{:S(2)}) async-start(), calls=%async_computation.34 | async-start | bytes 1572864 | tf_op jit(solution)/shard_map/all_gather | solution.py:25
  145.5 84.6 %reduce-scatter.35.cloned.1.call-start = ((), (), s32[]{:S(2)}) async-start(), calls=%async_computation.35 | async-start | bytes 5242880 | tf_op jit(solution)/shard_map/reduce_scatter | solution.py:27
  181.9 103.7 %all-gather.37.cloned.1.call-start = ((), (), s32[]{:S(2)}) async-start(), calls=%async_computation.36 | async-start | bytes 1572864 | tf_op jit(solution)/shard_map/all_gather | solution.py:25
  314.8 103.7 %all-gather.39.cloned.1.call-start = ((), (), s32[]{:S(2)}) async-start(), calls=%async_computation.38 | async-start | bytes 1572864 | tf_op jit(solution)/shard_map/all_gather | solution.py:25
  447.7 103.5 %all-gather.41.cloned.1.call-start = ((), (), s32[]{:S(2)}) async-start(), calls=%async_computation.40 | async-start | bytes 1572864 | tf_op jit(solution)/shard_map/all_gather | solution.py:25
  543.9 84.6 %reduce-scatter.41.cloned.1.call-start = ((), (), s32[]{:S(2)}) async-start(), calls=%async_computation.41 | async-start | bytes 5242880 | tf_op jit(solution)/shard_map/reduce_scatter | solution.py:27
  580.4 103.8 %all-gather.43.cloned.1.call-start = ((), (), s32[]{:S(2)}) async-start(), calls=%async_computation.42 | async-start | bytes 1572864 | tf_op jit(solution)/shard_map/all_gather | solution.py:25
  676.9 84.6 %reduce-scatter.43.cloned.1.call-start = ((), (), s32[]{:S(2)}) async-start(), calls=%async_computation.43 | async-start | bytes 5242880 | tf_op jit(solution)/shard_map/reduce_scatter | solution.py:27
  713.4 103.7 %all-gather.45.cloned.1.call-start = ((), (), s32[]{:S(2)}) async-start(), calls=%async_computation.44 | async-start | bytes 1572864 | tf_op jit(solution)/shard_map/all_gather | solution.py:25
  809.8 84.6 %reduce-scatter.45.cloned.1.call-start = ((), (), s32[]{:S(2)}) async-start(), calls=%async_computation.45 | async-start | bytes 5242880 | tf_op jit(solution)/shard_map/reduce_scatter | solution.py:27
  846.3 103.5 %all-gather.47.cloned.1.call-start = ((), (), s32[]{:S(2)}) async-start(), calls=%async_computation.46 | async-start | bytes 1572864 | tf_op jit(solution)/shard_map/all_gather | solution.py:25
  978.9 103.6 %all-gather.49.cloned.1.call-start = ((), (), s32[]{:S(2)}) async-start(), calls=%async_computation.48 | async-start | bytes 1572864 | tf_op jit(solution)/shard_map/all_gather | solution.py:25
  1111.7 103.7 %all-gather.51.cloned.1.call-start = ((), (), s32[]{:S(2)}) async-start(), calls=%async_computation.50 | async-start | bytes 1572864 | tf_op jit(solution)/shard_map/all_gather | solution.py:25
  1244.6 103.6 %all-gather.53.cloned.1.call-start = ((), (), s32[]{:S(2)}) async-start(), calls=%async_computation.52 | async-start | bytes 1572864 | tf_op jit(solution)/shard_map/all_gather | solution.py:25
  1341.0 84.6 %reduce-scatter.53.cloned.1.call-start = ((), (), s32[]{:S(2)}) async-start(), calls=%async_computation.53 | async-start | bytes 5242880 | tf_op jit(solution)/shard_map/reduce_scatter | solution.py:27
  1377.4 103.6 %all-gather.55.cloned.1.call-start = ((), (), s32[]{:S(2)}) async-start(), calls=%async_computation.54 | async-start | bytes 1572864 | tf_op jit(solution)/shard_map/all_gather | solution.py:25
  1473.8 84.6 %reduce-scatter.55.cloned.1.call-start = ((), (), s32[]{:S(2)}) async-start(), calls=%async_computation.55 | async-start | bytes 5242880 | tf_op jit(solution)/shard_map/reduce_scatter | solution.py:27
  1510.3 103.5 %all-gather.57.cloned.1.call-start = ((), (), s32[]{:S(2)}) async-start(), calls=%async_computation.56 | async-start | bytes 1572864 | tf_op jit(solution)/shard_map/all_gather | solution.py:25
  1606.6 84.6 %reduce-scatter.57.cloned.1.call-start = ((), (), s32[]{:S(2)}) async-start(), calls=%async_computation.57 | async-start | bytes 5242880 | tf_op jit(solution)/shard_map/reduce_scatter | solution.py:27
  1643.0 104.8 %all-gather.59.cloned.1.call-start = ((), (), s32[]{:S(2)}) async-start(), calls=%async_computation.58 | async-start | bytes 1572864 | tf_op jit(solution)/shard_map/all_gather | solution.py:25
  1740.5 84.6 %reduce-scatter.59.cloned.1.call-start = ((), (), s32[]{:S(2)}) async-start(), calls=%async_computation.59 | async-start | bytes 5242880 | tf_op jit(solution)/shard_map/reduce_scatter | solution.py:27
  1777.0 109.7 %all-gather.61.cloned.1.call-start = ((), (), s32[]{:S(2)}) async-start(), calls=%async_computation.60 | async-start | bytes 1572864 | tf_op jit(solution)/shard_map/all_gather | solution.py:25
  1915.9 103.5 %all-gather.63.cloned.1.call-start = ((), (), s32[]{:S(2)}) async-start(), calls=%async_computation.62 | async-start | bytes 1572864 | tf_op jit(solution)/shard_map/all_gather | solution.py:25
  2048.5 103.7 %all-gather.65.cloned.1.call-start = ((), (), s32[]{:S(2)}) async-start(), calls=%async_computation.64 | async-start | bytes 1572864 | tf_op jit(solution)/shard_map/all_gather | solution.py:25
  2181.5 103.8 %all-gather.67.cloned.1.call-start = ((), (), s32[]{:S(2)}) async-start(), calls=%async_computation.66 | async-start | bytes 1572864 | tf_op jit(solution)/shard_map/all_gather | solution.py:25
  2314.4 103.6 %all-gather.69.cloned.1.call-start = ((), (), s32[]{:S(2)}) async-start(), calls=%async_computation.68 | async-start | bytes 1572864 | tf_op jit(solution)/shard_map/all_gather | solution.py:25
  2447.2 103.7 %all-gather.71.cloned.1.call-start = ((), (), s32[]{:S(2)}) async-start(), calls=%async_computation.70 | async-start | bytes 1572864 | tf_op jit(solution)/shard_map/all_gather | solution.py:25
  2580.1 103.6 %all-gather.73.cloned.1.call-start = ((), (), s32[]{:S(2)}) async-start(), calls=%async_computation.72 | async-start | bytes 1572864 | tf_op jit(solution)/shard_map/all_gather | solution.py:25
  2713.0 103.6 %all-gather.75.cloned.1.call-start = ((), (), s32[]{:S(2)}) async-start(), calls=%async_computation.74 | async-start | bytes 1572864 | tf_op jit(solution)/shard_map/all_gather | solution.py:25
  2809.3 84.6 %reduce-scatter.75.cloned.1.call-start = ((), (), s32[]{:S(2)}) async-start(), calls=%async_computation.75 | async-start | bytes 5242880 | tf_op jit(solution)/shard_map/reduce_scatter | solution.py:27
  2845.7 103.7 %all-gather.77.cloned.1.call-start = ((), (), s32[]{:S(2)}) async-start(), calls=%async_computation.76 | async-start | bytes 1572864 | tf_op jit(solution)/shard_map/all_gather | solution.py:25
  2942.2 84.6 %reduce-scatter.77.cloned.1.call-start = ((), (), s32[]{:S(2)}) async-start(), calls=%async_computation.77 | async-start | bytes 5242880 | tf_op jit(solution)/shard_map/reduce_scatter | solution.py:27
  2978.6 103.6 %all-gather.79.cloned.1.call-start = ((), (), s32[]{:S(2)}) async-start(), calls=%async_computation.78 | async-start | bytes 1572864 | tf_op jit(solution)/shard_map/all_gather | solution.py:25
  3075.0 84.6 %reduce-scatter.79.cloned.1.call-start = ((), (), s32[]{:S(2)}) async-start(), calls=%async_computation.79 | async-start | bytes 5242880 | tf_op jit(solution)/shard_map/reduce_scatter | solution.py:27
  3111.4 103.5 %all-gather.81.cloned.1.call-start = ((), (), s32[]{:S(2)}) async-start(), calls=%async_computation.80 | async-start | bytes 1572864 | tf_op jit(solution)/shard_map/all_gather | solution.py:25
  3244.1 103.8 %all-gather.83.cloned.1.call-start = ((), (), s32[]{:S(2)}) async-start(), calls=%async_computation.82 | async-start | bytes 1572864 | tf_op jit(solution)/shard_map/all_gather | solution.py:25
  3340.6 84.6 %reduce-scatter.83.cloned.1.call-start = ((), (), s32[]{:S(2)}) async-start(), calls=%async_computation.83 | async-start | bytes 5242880 | tf_op jit(solution)/shard_map/reduce_scatter | solution.py:27
  3377.1 103.7 %all-gather.85.cloned.1.call-start = ((), (), s32[]{:S(2)}) async-start(), calls=%async_computation.84 | async-start | bytes 1572864 | tf_op jit(solution)/shard_map/all_gather | solution.py:25
  3473.6 84.6 %reduce-scatter.85.cloned.1.call-start = ((), (), s32[]{:S(2)}) async-start(), calls=%async_computation.85 | async-start | bytes 5242880 | tf_op jit(solution)/shard_map/reduce_scatter | solution.py:27
  3510.0 103.6 %all-gather.87.cloned.1.call-start = ((), (), s32[]{:S(2)}) async-start(), calls=%async_computation.86 | async-start | bytes 1572864 | tf_op jit(solution)/shard_map/all_gather | solution.py:25
  3606.3 84.6 %reduce-scatter.87.cloned.1.call-start = ((), (), s32[]{:S(2)}) async-start(), calls=%async_computation.87 | async-start | bytes 5242880 | tf_op jit(solution)/shard_map/reduce_scatter | solution.py:27
  3642.8 103.6 %all-gather.89.cloned.1.call-start = ((), (), s32[]{:S(2)}) async-start(), calls=%async_computation.88 | async-start | bytes 1572864 | tf_op jit(solution)/shard_map/all_gather | solution.py:25
  3739.2 84.6 %reduce-scatter.89.cloned.1.call-start = ((), (), s32[]{:S(2)}) async-start(), calls=%async_computation.89 | async-start | bytes 5242880 | tf_op jit(solution)/shard_map/reduce_scatter | solution.py:27
  3775.6 103.6 %all-gather.91.cloned.1.call-start = ((), (), s32[]{:S(2)}) async-start(), calls=%async_computation.90 | async-start | bytes 1572864 | tf_op jit(solution)/shard_map/all_gather | solution.py:25
  3908.4 103.6 %all-gather.93.cloned.1.call-start = ((), (), s32[]{:S(2)}) async-start(), calls=%async_computation.92 | async-start | bytes 1572864 | tf_op jit(solution)/shard_map/all_gather | solution.py:25
  4004.8 84.7 %reduce-scatter.93.cloned.1.call-start = ((), (), s32[]{:S(2)}) async-start(), calls=%async_computation.93 | async-start | bytes 5242880 | tf_op jit(solution)/shard_map/reduce_scatter | solution.py:27
  4041.4 104.7 %all-gather.95.cloned.1.call-start = ((), (), s32[]{:S(2)}) async-start(), calls=%async_computation.94 | async-start | bytes 1572864 | tf_op jit(solution)/shard_map/all_gather | solution.py:25
  (99 other events, 7207.0 us)
Sparse Core Ops, SparseCore 0:
  10.9 8.9 all-gather.32
  49.2 48.0 reduce-scatter.32
  182.1 48.0 reduce-scatter.34
  278.5 7.0 all-gather.36
  314.9 47.9 reduce-scatter.36
  447.8 47.9 reduce-scatter.38
  580.5 48.0 reduce-scatter.40
  713.5 48.0 reduce-scatter.42
  810.0 7.0 all-gather.44
  846.4 48.0 reduce-scatter.44
  979.0 48.0 reduce-scatter.46
  1111.9 48.0 reduce-scatter.48
  1244.8 48.0 reduce-scatter.50
  1341.1 7.0 all-gather.52
  1377.6 48.0 reduce-scatter.52
  1474.0 7.0 all-gather.54
  1510.4 48.0 reduce-scatter.54
  1643.1 48.0 reduce-scatter.56
  1740.7 7.0 all-gather.58
  1777.1 48.0 reduce-scatter.58
  1916.0 48.0 reduce-scatter.60
  2048.7 48.0 reduce-scatter.62
  2181.6 47.9 reduce-scatter.64
  2278.1 7.0 all-gather.66
  2314.5 47.9 reduce-scatter.66
  2410.9 7.0 all-gather.68
  2447.3 48.0 reduce-scatter.68
  2580.2 48.0 reduce-scatter.70
  2713.1 48.0 reduce-scatter.72
  2809.4 7.0 all-gather.74
  2845.9 48.0 reduce-scatter.74
  2942.3 7.0 all-gather.76
  2978.7 47.9 reduce-scatter.76
  3075.1 7.0 all-gather.78
  3111.5 47.9 reduce-scatter.78
  3244.2 48.0 reduce-scatter.80
  3340.8 7.0 all-gather.82
  3377.2 48.0 reduce-scatter.82
  3473.7 7.0 all-gather.84
  3510.1 48.0 reduce-scatter.84
  3606.5 7.0 all-gather.86
  3642.9 48.0 reduce-scatter.86
  3739.3 7.0 all-gather.88
  3775.7 48.0 reduce-scatter.88
  3908.5 47.9 reduce-scatter.90
  4004.9 7.0 all-gather.92
  4041.5 48.0 reduce-scatter.92
  4175.4 48.0 reduce-scatter.94
  (16 shorter events, 112.2 us)
where the time goes:
time: 4320 us; the launch traced here: 4310 us
  waiting for transfers between devices  1760 us (41%)
  blocking collectives  1340 us (31%)
  matrix products  933 us (22%)
  starting transfers between devices  102 us (2%)
  other arithmetic  100 us (2%)
    reduce_scatter x32, waiting for transfers between devices, sweeps(): lax.psum_scatter(partial_prod, 'col', scatter_dimension=0, tiled=True)  1540 us
    psum x32, blocking collectives, sweeps(): lax.psum(jnp.sum(jnp.where(dang_mask, x_cur, 0.0), axis=0), both_axes)  1320 us
    dot_general x32, matrix products, sweeps(): jnp.dot(adj_tile, x_source, preferred_element_type=jnp.float32)  933 us
    all_gather x32, waiting for transfers between devices, sweeps(): lax.all_gather(x_cur.astype(jnp.bfloat16), 'row', axis=0, tiled=True)  223 us
    ppermute x32, starting transfers between devices, sweeps(): moved = lax.ppermute(folded, both_axes, pairs)  90.2 us
  transfers between devices with their start and end apart: 96, of which 64 were waited for; matrix products, arithmetic and copies ran while one was open for 1% of the time, Pallas kernels for 0%

commit v1 on v0

v1 whole, which is shorter than its diff:
```python
import functools

import jax
import jax.numpy as jnp
from jax import lax
from jax.experimental import pallas as pl
from jax.experimental.pallas import tpu as pltpu
from jax.sharding import PartitionSpec as P

F32, BF16, F8 = jnp.float32, jnp.bfloat16, jnp.float8_e4m3fn
NT = (((1,), (1,)), ((), ()))
N_CHUNK = 8
N_SUB = N_CHUNK // 2
LANES = 128


def kernel(
    n_vert, n_step,
    b_hbm, x_hbm, v_ref, w_ref, dang_ref, damp_ref,
    xo_ref, res_ref,
    b_ref, far_out, near_out, rx, ry, fwd, y_ref, xb_out, xb_in, mass_out, mass_in, coef, racc, macc,
    load_sem, far_sem, near_sem, rx_sem, ry_sem, fwd_sem, xbs_sem, xbr_sem, ms_sem, mr_sem,
):
    c = lax.axis_index("col")
    i = lax.axis_index("row")
    half_m, chunk = far_out.shape[2], far_out.shape[3]
    half_rows = N_CHUNK * chunk
    c_x = c + 1 - 2 * (c % 2)
    c_y = (c + 2) % 4
    c_d = 3 - c
    x_nbr = {"col": c_x, "row": i}
    y_nbr = {"col": c_y, "row": i}
    mate = {"col": c, "row": 1 - i}
    peers = [x_nbr, {"col": c_y, "row": 1 - i}, {"col": c_d, "row": 1 - i}]
    role = (c // 2 + i) % 2
    keeps = role == 0
    far_row = (1 - c % 2) * half_rows
    near_row = (c % 2) * half_rows

    def remote(src, dst, send, recv, dev):
        return pltpu.make_async_remote_copy(
            src_ref=src, dst_ref=dst, send_sem=send, recv_sem=recv, device_id=dev, device_id_type=pl.DeviceIdType.MESH
        )

    def product(h, row):
        rows = pl.ds(pl.multiple_of(row, chunk), chunk)
        both = lax.dot_general(y_ref[h], b_ref[rows, :], NT, preferred_element_type=F32)
        return both[:half_m] + both[half_m:]

    def set_y(h, j, xb):
        prod = xb.astype(F32) * w_ref[j]
        high = prod.astype(BF16)
        low = (prod - high.astype(F32)).astype(BF16)
        cols = pl.ds(pl.multiple_of(j * chunk, chunk), chunk)
        y_ref[h, :half_m, cols] = high
        y_ref[h, half_m:, cols] = low

    def far_copy(par, h, n, dev):
        return remote(far_out.at[h, n], rx.at[par, h, n], far_sem.at[h, n], rx_sem.at[par, h, n], dev)

    def hop_copy(par, h, n, k, dev):
        return remote(far_out.at[h, n], fwd.at[par, h, k], far_sem.at[h, n], fwd_sem.at[par, h, k], dev)

    def near_copy(par, h, n):
        return remote(near_out.at[h, n], ry.at[par, h, n], near_sem.at[h, n], ry_sem.at[par, h, n], y_nbr)

    def xb_copy(par, h, j):
        return remote(xb_out.at[h, j], xb_in.at[par, h, j], xbs_sem.at[h, j], xbr_sem.at[par, h, j], mate)

    def mass_copy(par, h, k):
        return remote(mass_out.at[h], mass_in.at[par, h, k], ms_sem.at[h, k], mr_sem.at[par, h, k], peers[k])

    def far(t, par, h, lo, hi):
        def step(it, carry):
            sub = (1 - role) * (it // N_SUB) + role * (1 - it % 2)
            k = (1 - role) * (it % N_SUB) + role * (it // 2)
            n = sub * N_SUB + k
            got = product(h, far_row + n * chunk)

            @pl.when(t > 0)
            def _():
                far_copy(par, h, n, x_nbr).wait_send()

            @pl.when(jnp.logical_and(keeps, sub == 1))
            def _():
                hop_copy(par, h, n, k, y_nbr).wait_recv()
                far_out[h, n] = got + fwd[par, h, k]

            @pl.when(jnp.logical_not(jnp.logical_and(keeps, sub == 1)))
            def _():
                far_out[h, n] = got

            @pl.when(keeps)
            def _():
                far_copy(par, h, n, x_nbr).start()

            @pl.when(jnp.logical_not(keeps))
            def _():
                dev = {"col": (1 - sub) * c_x + sub * c_y, "row": i}
                hop_copy(par, h, n, k, dev).start()

            return carry

        lax.fori_loop(lo, hi, step, 0)

    def near(t, par, h):
        def step(it, carry):
            sub = 1 - it // N_SUB
            k = it % N_SUB
            n = sub * N_SUB + k
            got = product(h, near_row + n * chunk)

            @pl.when(keeps)
            def _():
                near_out[h, n] = got

            @pl.when(jnp.logical_not(keeps))
            def _():
                @pl.when(t > 0)
                def _():
                    near_copy(par, h, n).wait_send()

                @pl.when(sub == 0)
                def _():
                    hop_copy(par, h, n, k, x_nbr).wait_recv()
                    near_out[h, n] = got + fwd[par, h, k]

                @pl.when(sub == 1)
                def _():
                    near_out[h, n] = got

                near_copy(par, h, n).start()

            return carry

        lax.fori_loop(0, N_CHUNK, step, 0)

    def lane_sums(acc):
        return jnp.sum(acc[...].T, axis=0, keepdims=True)

    def send_mass(par, h):
        mass_out[h] = jnp.broadcast_to(lane_sums(macc), mass_out.shape[1:])
        for k in range(3):
            mass_copy(par, h, k).start()

    def finalise(t, h):
        par = t % 2
        d = damp_ref[t]
        mass = mass_out[h]
        for k in range(3):
            mass_copy(par, h, k).wait()
            mass = mass + mass_in[par, h, k]
        spread = jnp.broadcast_to(mass[0:1], (LANES, LANES)).T
        coef[...] = d * spread[:half_m] / n_vert + (1.0 - d)
        racc[...] = jnp.zeros_like(racc)
        macc[...] = jnp.zeros_like(macc)

        def step(j, carry):
            far_copy(par, h, j, x_nbr).wait_recv()
            near_copy(par, h, j).wait_recv()

            @pl.when(t > 0)
            def _():
                xb_copy(par, h, j).wait_send()

            r_sum = racc[:half_m, :]
            m_sum = macc[:half_m, :]
            for g in range(chunk // LANES):
                at = pl.ds(g * LANES, LANES)
                total = near_out[h, j, :, at] + rx[par, h, j, :, at] + ry[par, h, j, :, at]
                new = d * total + coef[...] * v_ref[h, j, :, at]
                r_sum = r_sum + jnp.abs(new - xo_ref[h, j, :, at])
                m_sum = m_sum + jnp.where(dang_ref[j, :, at] > 0, new, 0.0)
                xo_ref[h, j, :, at] = new
                xb_out[h, j, :, at] = new.astype(BF16)
            racc[:half_m, :] = r_sum
            macc[:half_m, :] = m_sum

            @pl.when(t < n_step - 1)
            def _():
                xb_copy(1 - par, h, j).start()
                set_y(h, j, xb_out[h, j])

            return carry

        lax.fori_loop(0, N_CHUNK, step, 0)
        res_ref[h, pl.ds(t, 1), :] = lane_sums(racc) / n_vert

        @pl.when(t < n_step - 1)
        def _():
            send_mass(1 - par, h)

    b_load = pltpu.make_async_copy(b_hbm, b_ref, load_sem.at[0])
    x_load = pltpu.make_async_copy(x_hbm, xo_ref, load_sem.at[1])
    b_load.start()
    x_load.start()
    res_ref[...] = jnp.zeros_like(res_ref)
    x_load.wait()
    for h in range(2):
        def first(j, carry, h=h):
            set_y(h, j, xo_ref[h, j].astype(BF16))
            return carry

        lax.fori_loop(0, N_CHUNK, first, 0)

        @pl.when(keeps)
        def _(h=h):
            macc[...] = jnp.zeros_like(macc)

            def add(j, carry):
                m_sum = macc[:half_m, :]
                for g in range(chunk // LANES):
                    at = pl.ds(g * LANES, LANES)
                    m_sum = m_sum + jnp.where(dang_ref[j, :, at] > 0, xo_ref[h, j, :, at], 0.0)
                macc[:half_m, :] = m_sum
                return carry

            lax.fori_loop(0, N_CHUNK, add, 0)
            send_mass(0, h)

    b_load.wait()

    def sweep(t, carry):
        par = t % 2
        for h in range(2):
            @pl.when(jnp.logical_and(jnp.logical_not(keeps), t > 0))
            def _(h=h):
                def take(j, carry):
                    xb_copy(par, h, j).wait_recv()
                    set_y(h, j, xb_in[par, h, j])
                    return carry

                lax.fori_loop(0, N_CHUNK, take, 0)

            far(t, par, h, 0, N_SUB)
            if h == 0:
                @pl.when(jnp.logical_and(keeps, t > 0))
                def _():
                    finalise(t - 1, 1)
            else:
                @pl.when(keeps)
                def _():
                    finalise(t, 0)
            far(t, par, h, N_SUB, N_CHUNK)
            near(t, par, h)
        return carry

    lax.fori_loop(0, n_step, sweep, 0)

    @pl.when(keeps)
    def _():
        finalise(n_step - 1, 1)

    last = (n_step - 1) % 2
    for h in range(2):
        def drain(n, carry, h=h):
            far_copy(last, h, n, x_nbr).wait_send()

            @pl.when(jnp.logical_not(keeps))
            def _():
                near_copy(last, h, n).wait_send()

            return carry

        lax.fori_loop(0, N_CHUNK, drain, 0)


def solution(mesh):
    swap = [(0, 1), (1, 0)]

    def sweeps(adj_tile, x_piece, tele_piece, dang_piece, damping):
        tile_rows, tile_cols = adj_tile.shape
        piece, m = x_piece.shape
        n_vert = tile_rows * mesh.shape["row"]
        n_step = damping.shape[0]
        chunk, half_m = tile_cols // N_CHUNK, m // 2
        i = lax.axis_index("row")

        def both(own):
            other = lax.ppermute(own, "row", swap)
            return jnp.where(i == 0, jnp.concatenate([own, other]), jnp.concatenate([other, own]))

        def chunks(a):
            return a.reshape(N_CHUNK, chunk, 2, half_m).transpose(2, 0, 3, 1)

        top = jnp.max(adj_tile, axis=0).astype(F32)
        weight = jnp.maximum(top, lax.ppermute(top, "row", swap)).reshape(N_CHUNK, 1, chunk)
        edges = jnp.where(adj_tile > 0, 1.0, 0.0).astype(F8)
        x_in = chunks(both(x_piece))
        tele = chunks(both(tele_piece))
        dang = both(dang_piece).astype(F32).reshape(N_CHUNK, 1, chunk)

        part = (2, N_CHUNK, half_m, chunk)
        dma = pltpu.SemaphoreType.DMA
        vmem = pl.BlockSpec(memory_space=pltpu.VMEM)
        hbm = pl.BlockSpec(memory_space=pl.ANY)
        x_out, resid = pl.pallas_call(
            functools.partial(kernel, n_vert, n_step),
            out_shape=(jax.ShapeDtypeStruct(part, F32), jax.ShapeDtypeStruct((2, n_step, LANES), F32)),
            in_specs=[hbm, hbm, vmem, vmem, vmem, pl.BlockSpec(memory_space=pltpu.SMEM)],
            out_specs=(vmem, vmem),
            scratch_shapes=[
                pltpu.VMEM((tile_rows, tile_cols), F8),
                pltpu.VMEM(part, F32),
                pltpu.VMEM(part, F32),
                pltpu.VMEM((2, *part), F32),
                pltpu.VMEM((2, *part), F32),
                pltpu.VMEM((2, 2, N_SUB, half_m, chunk), F32),
                pltpu.VMEM((2, m, tile_cols), BF16),
                pltpu.VMEM(part, BF16),
                pltpu.VMEM((2, *part), BF16),
                pltpu.VMEM((2, 8, LANES), F32),
                pltpu.VMEM((2, 2, 3, 8, LANES), F32),
                pltpu.VMEM((half_m, LANES), F32),
                pltpu.VMEM((LANES, LANES), F32),
                pltpu.VMEM((LANES, LANES), F32),
                dma((2,)),
                dma((2, N_CHUNK)),
                dma((2, N_CHUNK)),
                dma((2, 2, N_CHUNK)),
                dma((2, 2, N_CHUNK)),
                dma((2, 2, N_SUB)),
                dma((2, N_CHUNK)),
                dma((2, 2, N_CHUNK)),
                dma((2, 3)),
                dma((2, 2, 3)),
            ],
            compiler_params=pltpu.CompilerParams(vmem_limit_bytes=67043328, has_side_effects=True),
            name="sweeps",
        )(edges, x_in, tele, weight, dang, damping)

        pieces = x_out.transpose(1, 3, 0, 2).reshape(2, piece, m)
        other = lax.ppermute(lax.dynamic_index_in_dim(pieces, 1 - i, 0, False), "row", swap)
        keeps = lax.axis_index("col") // 2 == i
        x_final = jnp.where(keeps, lax.dynamic_index_in_dim(pieces, i, 0, False), other)
        resid = lax.psum(resid[:, :, :half_m].transpose(1, 0, 2).reshape(n_step, m), ("col", "row"))
        return x_final, resid

    vec_spec = P(("col", "row"), None)
    return jax.shard_map(
        sweeps, mesh=mesh, in_specs=(P("row", "col"), vec_spec, vec_spec, P(("col", "row")), P()), out_specs=(vec_spec, P()), check_vma=False
    )
```

time: 4320 us -> 1250 us (0.29)
  waiting for transfers between devices: 1760 us -> 0.01 us
  blocking collectives: 1340 us -> 22.2 us
  Pallas kernels: 0 us -> 1110 us
  matrix products: 933 us -> 0 us
  starting transfers between devices: 102 us -> 1.47 us
    reduce_scatter x32 -> x0, waiting for transfers between devices: 1540 us -> none  [sweeps(): lax.psum_scatter(partial_prod, 'col', scatter_dimension=0, tiled=True)]
    psum x33 -> x1, blocking collectives: 1340 us -> 22.2 us  [sweeps(): lax.psum(resid[:, :, :half_m].transpose(1, 0, 2).reshape(n_step, m), ('co...]
    pallas_call x0 -> x1, Pallas kernels: none -> 1110 us  [sweeps(): pl.pallas_call(functools.partial(kernel, n_vert, n_step), out_shape=(jax....]
    dot_general x32 -> x0, matrix products: 933 us -> none  [sweeps(): jnp.dot(adj_tile, x_source, preferred_element_type=jnp.float32)]
    all_gather x32 -> x0, waiting for transfers between devices: 223 us -> none  [sweeps(): lax.all_gather(x_cur.astype(jnp.bfloat16), 'row', axis=0, tiled=True)]
    ppermute x32 -> x5, starting transfers between devices: 90.2 us -> 1.47 us  [the longest x3 1.39 us: both(): other = lax.ppermute(own, 'row', swap)]
    reduce_sum x32 -> x0, other arithmetic: 50.3 us -> none  [the longest x30 34.4 us: sweeps(): jnp.sum(jnp.where(dang_mask, x_cur, 0.0), axis=0)]
  transfers between devices with their start and end apart: 96 -> 5, of which waited for: 64 -> 0; matrix products, arithmetic and copies ran while one was open for 1% -> 6% of each run, Pallas kernels for 0% -> 0%
where the time goes in v1:
time: 1250 us
  Pallas kernels  1110 us (89%)
  other arithmetic  76.1 us (6%)
  local copies, waits for them, and re-layouts  37.1 us (3%)
  blocking collectives  22.2 us (2%)
    pallas_call x1, Pallas kernels, sweeps(): pl.pallas_call(functools.partial(kernel, n_vert, n_step), out_shape=(jax....  1110 us
    reduce_max x1, other arithmetic, sweeps(): top = jnp.max(adj_tile, axis=0).astype(F32)  36.5 us
    convert_element_type x1, other arithmetic, sweeps(): edges = jnp.where(adj_tile > 0, 1.0, 0.0).astype(F8)  32.7 us
  transfers between devices with their start and end apart: 5, of which 0 were waited for; matrix products, arithmetic and copies ran while one was open for 6% of the time, Pallas kernels for 0%

profile of v1, /device:TPU:0, one launch (start us, length us, event | category | flops | bytes accessed | tf_op | source)
XLA Modules:
  0.0 1247.4 jit_solution(14574292989817771215)
XLA Ops:
  0.6 0.9 collective-permute-start
  1.5 0.0 collective-permute-start.1
  1.5 0.5 collective-permute-start.3
  2.0 36.5 %reduce_max.9 = bf16[4096]{0:T(1024)(128)(2,1)S(1)} reduce(bf16[8192,4096]{1,0:T(8,128)(2,1)} %param.5, bf16[]{:T(256)} %constant.38.clone.1), dimensions={0}, to_apply=%region_0.0 | reduce | flops 33550336 | bytes 67117056 | tf_op jit(solution)/shard_map/reduce_max | solution.py:286
  38.5 0.0 copy-start.3
  38.5 0.0 copy-start
  38.5 0.1 collective-permute-start.2
  38.6 32.7 %select_convert_fusion.b_hbm = f8e4m3fn[8192,4096]{1,0:T(32,128)(4,1)} fusion(bf16[8192,4096]{1,0:T(8,128)(2,1)} %param.5), kind=kLoop, calls=%fused_computation | loop fusion | flops 100663296 | bytes 100663296 | tf_op jit(solution)/shard_map/convert_element_type | solution.py:288
  71.3 0.0 collective-permute-done.3
  71.3 0.0 copy-done.3
  71.4 0.6 fusion.dang_ref
  72.0 0.0 collective-permute-done.2
  72.0 0.6 convert_maximum_fusion
  72.6 0.0 collective-permute-done
  72.6 0.0 copy-start.1
  72.6 1.0 copy-done.1
  73.6 0.0 collective-permute-done.1
  73.6 0.0 copy-done
  73.6 4.5 maximum_select_fusion
  78.1 5.6 reshape.85
  83.7 6.7 copy.14
  90.4 3.7 reshape.86
  94.1 6.7 copy.16
  100.8 1109.7 %sweeps.1 = (f32[2,8,64,512]{3,2,1,0:T(8,128)}, f32[2,32,128]{2,1,0:T(8,128)}) custom-call(f8e4m3fn[8192,4096]{1,0:T(32,128)(4,1)} %select_convert_fusion.b_hbm, f32[2,8,64,512]{3,2,1,0:T(8,128)} %bitcast.15, f32[2,8,64,512]{3,2,1,0:T(8,128)} %bitcast.16, f32[8,1,512]{2,1,0:T(1,128)} %bitcast.19, f32[8,1,512]{2,1,0:T(1,128)} %fusion.dang_ref, f32[32]{0:T(128)} %damp_ref.1), custom_call_target="tpu_custom_call" | custom-call | tf_op jit(solution)/shard_map/sweeps/pallas_call | solution.py:297
  1210.6 4.2 copy.17
  1214.7 2.9 reshape.83
  1217.6 3.1 constant_dynamic-slice_fusion.1
  1220.8 0.0 copy-start.2
  1220.8 2.3 copy.19
  1223.1 0.0 collective-permute-start.4
  1223.2 0.7 copy.18
  1223.9 0.0 copy-done.2
  1224.0 0.1 reshape.84
  1224.1 22.2 %psum.7 = f32[32,128]{1,0:T(8,128)} all-reduce(f32[32,128]{1,0:T(8,128)S(1)} %reshape.84), channel_id=1, replica_groups=mesh['col'=4,'row'=2] {'col','row'}, use_global_device_ids=true, to_apply=%region_1.2 | all-reduce | flops 4096 | bytes 32768 | tf_op jit(solution)/shard_map/psum | solution.py:336
  1246.3 0.0 collective-permute-done.4
  1246.3 1.1 bitcast_select_fusion
  (3 shorter events, 0.0 us)
Async XLA Ops:
  0.6 72.0 %collective-permute-start = (f32[2048,128]{1,0:T(8,128)}, f32[2048,128]{1,0:T(8,128)S(1)}, u32[]{:S(2)}, u32[]{:S(2)}) collective-permute-start(f32[2048,128]{1,0:T(8,128)} %param.6), channel_id=1, source_target_pairs={{0,1},{1,0},{2,3},{3,2},{4,5},{5,4},{6,7},{7,6}} | collective-permute-start | bytes 3145736 | tf_op jit(solution)/shard_map/ppermute | solution.py:280
  1.5 72.1 %collective-permute-start.1 = (f32[2048,128]{1,0:T(8,128)}, f32[2048,128]{1,0:T(8,128)}, u32[]{:S(2)}, u32[]{:S(2)}) collective-permute-start(f32[2048,128]{1,0:T(8,128)} %param.7), channel_id=1, source_target_pairs={{0,1},{1,0},{2,3},{3,2},{4,5},{5,4},{6,7},{7,6}} | collective-permute-start | bytes 3145736 | tf_op jit(solution)/shard_map/ppermute | solution.py:280
  1.5 69.8 %collective-permute-start.3 = (s32[2048]{0:T(1024)}, s32[2048]{0:T(1024)S(1)}, u32[]{:S(2)}, u32[]{:S(2)}) collective-permute-start(s32[2048]{0:T(1024)} %param.8), channel_id=1, source_target_pairs={{0,1},{1,0},{2,3},{3,2},{4,5},{5,4},{6,7},{7,6}} | collective-permute-start | bytes 24584 | tf_op jit(solution)/shard_map/ppermute | solution.py:280
  38.5 32.8 %copy-start.3 = (s32[2048]{0:T(1024)S(1)}, s32[2048]{0:T(1024)}, u32[]{:S(2)}) copy-start(s32[2048]{0:T(1024)} %param.8) | copy-start | bytes 24580
  38.5 35.0 %copy-start = (f32[2048,128]{1,0:T(8,128)S(1)}, f32[2048,128]{1,0:T(8,128)}, u32[]{:S(2)}) copy-start(f32[2048,128]{1,0:T(8,128)} %param.6) | copy-start | bytes 3145732
  38.5 33.4 %collective-permute-start.2 = (f32[4096]{0:T(1024)S(1)}, f32[4096]{0:T(1024)S(1)}, u32[]{:S(2)}, u32[]{:S(2)}) collective-permute-start(f32[4096]{0:T(1024)S(1)} %convert_element_type.17), channel_id=1, source_target_pairs={{0,1},{1,0},{2,3},{3,2},{4,5},{5,4},{6,7},{7,6}} | collective-permute-start | bytes 49160 | tf_op jit(solution)/shard_map/ppermute | solution.py:287
  72.6 1.0 copy-start.1
  1220.8 3.2 copy-start.2
  1223.1 23.2 %collective-permute-start.4 = (f32[2048,128]{1,0:T(8,128)S(1)}, f32[2048,128]{1,0:T(8,128)}, u32[]{:S(2)}, u32[]{:S(2)}) collective-permute-start(f32[2048,128]{1,0:T(8,128)S(1)} %bitcast.18), channel_id=1, source_target_pairs={{0,1},{1,0},{2,3},{3,2},{4,5},{5,4},{6,7},{7,6}} | collective-permute-start | bytes 3145736 | tf_op jit(solution)/shard_map/ppermute | solution.py:333

commit v2 on v1

--- a/solution.py
+++ b/solution.py
@@ -16,10 +16,12 @@
 
 def kernel(
     n_vert, n_step,
-    b_hbm, x_hbm, v_ref, w_ref, dang_ref, damp_ref,
-    xo_ref, res_ref,
+    a_hbm, x_hbm, v_hbm, dang_in, damp_ref,
+    out_ref, res_ref,
+    xo_ref, v_ref, dang_ref,
     b_ref, far_out, near_out, rx, ry, fwd, y_ref, xb_out, xb_in, mass_out, mass_in, coef, racc, macc,
-    load_sem, far_sem, near_sem, rx_sem, ry_sem, fwd_sem, xbs_sem, xbr_sem, ms_sem, mr_sem,
+    stage, w_own, w_in, w_ref, res_all, first_out,
+    load_sem, w_sem, res_sem, ex_sem, end_sem, far_sem, near_sem, rx_sem, ry_sem, fwd_sem, xbs_sem, xbr_sem, ms_sem, mr_sem,
 ):
     c = lax.axis_index("col")
     i = lax.axis_index("row")
@@ -70,17 +72,27 @@
     def mass_copy(par, h, k):
         return remote(mass_out.at[h], mass_in.at[par, h, k], ms_sem.at[h, k], mr_sem.at[par, h, k], peers[k])
 
-    def far(t, par, h, lo, hi):
+    def far_place(it):
+        sub = (1 - role) * (it // N_SUB) + role * (1 - it % 2)
+        k = (1 - role) * (it % N_SUB) + role * (it // 2)
+        return sub, k, sub * N_SUB + k
+
+    def near_place(it):
+        sub = 1 - it // N_SUB
+        k = it % N_SUB
+        return sub, k, sub * N_SUB + k
+
+    def far(par, h, lo, hi):
         def step(it, carry):
-            sub = (1 - role) * (it // N_SUB) + role * (1 - it % 2)
-            k = (1 - role) * (it % N_SUB) + role * (it // 2)
-            n = sub * N_SUB + k
+            sub, k, n = far_place(it)
             got = product(h, far_row + n * chunk)
-
-            @pl.when(t > 0)
-            def _():
-                far_copy(par, h, n, x_nbr).wait_send()
-
+            far_copy(par, h, n, x_nbr).wait_send()
+            emit_far(par, h, sub, k, n, got)
+            return carry
+
+        lax.fori_loop(lo, hi, step, 0)
+
+    def emit_far(par, h, sub, k, n, got):
             @pl.when(jnp.logical_and(keeps, sub == 1))
             def _():
                 hop_copy(par, h, n, k, y_nbr).wait_recv()
@@ -99,27 +111,28 @@
                 dev = {"col": (1 - sub) * c_x + sub * c_y, "row": i}
                 hop_copy(par, h, n, k, dev).start()
 
-            return carry
-
-        lax.fori_loop(lo, hi, step, 0)
-
-    def near(t, par, h):
+    def near(par, h):
         def step(it, carry):
-            sub = 1 - it // N_SUB
-            k = it % N_SUB
-            n = sub * N_SUB + k
+            sub, k, n = near_place(it)
             got = product(h, near_row + n * chunk)
 
+            @pl.when(jnp.logical_not(keeps))
+            def _():
+                near_copy(par, h, n).wait_send()
+
+            emit_near(par, h, sub, k, n, got)
+            return carry
+
+        lax.fori_loop(0, N_CHUNK, step, 0)
+
+    def emit_near(par, h, sub, k, n, got):
+
             @pl.when(keeps)
             def _():
                 near_out[h, n] = got
 
             @pl.when(jnp.logical_not(keeps))
             def _():
-                @pl.when(t > 0)
-                def _():
-                    near_copy(par, h, n).wait_send()
-
                 @pl.when(sub == 0)
                 def _():
                     hop_copy(par, h, n, k, x_nbr).wait_recv()
@@ -130,10 +143,6 @@
                     near_out[h, n] = got
 
                 near_copy(par, h, n).start()
-
-            return carry
-
-        lax.fori_loop(0, N_CHUNK, step, 0)
 
     def lane_sums(acc):
         return jnp.sum(acc[...].T, axis=0, keepdims=True)
@@ -184,21 +193,56 @@
             return carry
 
         lax.fori_loop(0, N_CHUNK, step, 0)
-        res_ref[h, pl.ds(t, 1), :] = lane_sums(racc) / n_vert
+        res_all[c, h, pl.ds(t, 1), :] = lane_sums(racc) / n_vert
 
         @pl.when(t < n_step - 1)
         def _():
             send_mass(1 - par, h)
 
-    b_load = pltpu.make_async_copy(b_hbm, b_ref, load_sem.at[0])
-    x_load = pltpu.make_async_copy(x_hbm, xo_ref, load_sem.at[1])
-    b_load.start()
-    x_load.start()
-    res_ref[...] = jnp.zeros_like(res_ref)
-    x_load.wait()
+    half = stage.shape[1]
+    per = chunk // half
+
+    def a_load(it):
+        slab = it // per
+        late = slab // N_CHUNK
+        n_far, n_near = far_place(slab % N_CHUNK)[2], near_place(slab % N_CHUNK)[2]
+        row = (1 - late) * (far_row + n_far * chunk) + late * (near_row + n_near * chunk)
+        row = pl.multiple_of(row + (it % per) * half, half)
+        return row, pltpu.make_async_copy(a_hbm.at[pl.ds(row, half), :], stage.at[it % 2], load_sem.at[it % 2])
+
+    a_load(0)[1].start()
+    w_own[...] = jnp.zeros_like(w_own)
+    own = pl.ds(i * N_SUB, N_SUB)
+    other = pl.ds((1 - i) * N_SUB, N_SUB)
+
+    def swap(ref, k):
+        return remote(ref, ref, ex_sem.at[0, k], ex_sem.at[1, k], mate)
+
+    swaps = []
+    for src, dst in ((x_hbm, xo_ref), (v_hbm, v_ref)):
+        load = pltpu.make_async_copy(src, out_ref, load_sem.at[2])
+        load.start()
+        load.wait()
+
+        def turn(n, carry, dst=dst):
+            block = out_ref[pl.ds(pl.multiple_of(n * chunk, chunk), chunk), :].T
+            dst[0, i * N_SUB + n] = block[:half_m]
+            dst[1, i * N_SUB + n] = block[half_m:]
+            return carry
+
+        lax.fori_loop(0, N_SUB, turn, 0)
+        for h in range(2):
+            swaps.append(swap(dst.at[h, own], len(swaps)))
+            swaps[-1].start()
+    dang_ref[own] = dang_in[...]
+    swaps.append(swap(dang_ref.at[own], len(swaps)))
+    swaps[-1].start()
+    for copy in swaps:
+        copy.wait()
     for h in range(2):
         def first(j, carry, h=h):
-            set_y(h, j, xo_ref[h, j].astype(BF16))
+            cols = pl.ds(pl.multiple_of(j * chunk, chunk), chunk)
+            y_ref[0, h * half_m : (h + 1) * half_m, cols] = xo_ref[h, j].astype(BF16)
             return carry
 
         lax.fori_loop(0, N_CHUNK, first, 0)
@@ -218,12 +262,46 @@
             lax.fori_loop(0, N_CHUNK, add, 0)
             send_mass(0, h)
 
-    b_load.wait()
+    def slab(n_slab, emit, place):
+        def step(it, carry):
+            for e in range(per):
+                at = (n_slab + it) * per + e
+                row, load = a_load(at)
+                load.wait()
+
+                @pl.when(at + 1 < 2 * N_CHUNK * per)
+                def _():
+                    a_load(at + 1)[1].start()
+
+                got = lax.dot_general(y_ref[0], stage[at % 2], NT, preferred_element_type=F32)
+                first_out[:, e * half : (e + 1) * half] = got
+                for j in range(N_CHUNK):
+                    cols = slice(j * chunk, (j + 1) * chunk)
+                    block = stage[at % 2, :, cols].astype(F32)
+                    w_own[j] = jnp.maximum(w_own[j], jnp.max(block, axis=0, keepdims=True))
+                    b_ref[pl.ds(row, half), cols] = jnp.where(block > 0, 1.0, 0.0).astype(F8)
+            sub, k, n = place(it)
+            for h in range(2):
+                emit(0, h, sub, k, n, first_out[h * half_m : (h + 1) * half_m, :])
+            return carry
+
+        lax.fori_loop(0, N_CHUNK, step, 0)
+
+    slab(0, emit_far, far_place)
+    slab(N_CHUNK, emit_near, near_place)
+    w_copy = remote(w_own, w_in, w_sem.at[0], w_sem.at[1], mate)
+    w_copy.start()
+    w_copy.wait()
+    w_ref[...] = jnp.maximum(w_own[...], w_in[...])
+
+    @pl.when(keeps)
+    def _():
+        finalise(0, 0)
 
     def sweep(t, carry):
         par = t % 2
         for h in range(2):
-            @pl.when(jnp.logical_and(jnp.logical_not(keeps), t > 0))
+            @pl.when(jnp.logical_not(keeps))
             def _(h=h):
                 def take(j, carry):
                     xb_copy(par, h, j).wait_recv()
@@ -232,20 +310,17 @@
 
                 lax.fori_loop(0, N_CHUNK, take, 0)
 
-            far(t, par, h, 0, N_SUB)
-            if h == 0:
-                @pl.when(jnp.logical_and(keeps, t > 0))
-                def _():
-                    finalise(t - 1, 1)
-            else:
-                @pl.when(keeps)
-                def _():
-                    finalise(t, 0)
-            far(t, par, h, N_SUB, N_CHUNK)
-            near(t, par, h)
+            far(par, h, 0, N_SUB)
+
+            @pl.when(keeps)
+            def _(h=h):
+                finalise(t - 1 + h, 1 - h)
+
+            far(par, h, N_SUB, N_CHUNK)
+            near(par, h)
         return carry
 
-    lax.fori_loop(0, n_step, sweep, 0)
+    lax.fori_loop(1, n_step, sweep, 0)
 
     @pl.when(keeps)
     def _():
@@ -264,42 +339,70 @@
 
         lax.fori_loop(0, N_CHUNK, drain, 0)
 
+    def end_copy(h, piece):
+        return remote(xo_ref.at[h, piece], xo_ref.at[h, piece], end_sem.at[0, h], end_sem.at[1, h], mate)
+
+    @pl.when(keeps)
+    def _():
+        for h in range(2):
+            end_copy(h, other).start()
+        for h in range(2):
+            end_copy(h, other).wait_send()
+
+    @pl.when(jnp.logical_not(keeps))
+    def _():
+        for h in range(2):
+            end_copy(h, own).wait_recv()
+
+    def turn_back(n, carry):
+        block = jnp.concatenate([xo_ref[0, i * N_SUB + n], xo_ref[1, i * N_SUB + n]], axis=0)
+        out_ref[pl.ds(pl.multiple_of(n * chunk, chunk), chunk), :] = block.T
+        return carry
+
+    lax.fori_loop(0, N_SUB, turn_back, 0)
+
+    def res_copy(k):
+        return remote(res_all.at[c], res_all.at[c], res_sem.at[k], res_sem.at[3 + k], peers[k])
+
+    total_copy = remote(res_ref, res_ref, res_sem.at[6], res_sem.at[7], mate)
+
+    @pl.when(keeps)
+    def _():
+        for k in range(3):
+            res_copy(k).start()
+        for k in range(3):
+            res_copy(k).wait()
+        res_ref[...] = res_all[0] + res_all[1] + res_all[2] + res_all[3]
+        total_copy.start()
+        total_copy.wait_send()
+
+    @pl.when(jnp.logical_not(keeps))
+    def _():
+        total_copy.wait_recv()
+
 
 def solution(mesh):
-    swap = [(0, 1), (1, 0)]
-
     def sweeps(adj_tile, x_piece, tele_piece, dang_piece, damping):
         tile_rows, tile_cols = adj_tile.shape
         piece, m = x_piece.shape
         n_vert = tile_rows * mesh.shape["row"]
         n_step = damping.shape[0]
         chunk, half_m = tile_cols // N_CHUNK, m // 2
-        i = lax.axis_index("row")
-
-        def both(own):
-            other = lax.ppermute(own, "row", swap)
-            return jnp.where(i == 0, jnp.concatenate([own, other]), jnp.concatenate([other, own]))
-
-        def chunks(a):
-            return a.reshape(N_CHUNK, chunk, 2, half_m).transpose(2, 0, 3, 1)
-
-        top = jnp.max(adj_tile, axis=0).astype(F32)
-        weight = jnp.maximum(top, lax.ppermute(top, "row", swap)).reshape(N_CHUNK, 1, chunk)
-        edges = jnp.where(adj_tile > 0, 1.0, 0.0).astype(F8)
-        x_in = chunks(both(x_piece))
-        tele = chunks(both(tele_piece))
-        dang = both(dang_piece).astype(F32).reshape(N_CHUNK, 1, chunk)
+        dang = dang_piece.astype(F32).reshape(N_SUB, 1, chunk)
 
         part = (2, N_CHUNK, half_m, chunk)
         dma = pltpu.SemaphoreType.DMA
         vmem = pl.BlockSpec(memory_space=pltpu.VMEM)
         hbm = pl.BlockSpec(memory_space=pl.ANY)
-        x_out, resid = pl.pallas_call(
+        x_final, resid = pl.pallas_call(
             functools.partial(kernel, n_vert, n_step),
-            out_shape=(jax.ShapeDtypeStruct(part, F32), jax.ShapeDtypeStruct((2, n_step, LANES), F32)),
-            in_specs=[hbm, hbm, vmem, vmem, vmem, pl.BlockSpec(memory_space=pltpu.SMEM)],
+            out_shape=(jax.ShapeDtypeStruct((piece, m), F32), jax.ShapeDtypeStruct((2, n_step, LANES), F32)),
+            in_specs=[hbm, hbm, hbm, vmem, pl.BlockSpec(memory_space=pltpu.SMEM)],
             out_specs=(vmem, vmem),
             scratch_shapes=[
+                pltpu.VMEM(part, F32),
+                pltpu.VMEM(part, F32),
+                pltpu.VMEM((N_CHUNK, 1, chunk), F32),
                 pltpu.VMEM((tile_rows, tile_cols), F8),
                 pltpu.VMEM(part, F32),
                 pltpu.VMEM(part, F32),
@@ -314,7 +417,17 @@
                 pltpu.VMEM((half_m, LANES), F32),
                 pltpu.VMEM((LANES, LANES), F32),
                 pltpu.VMEM((LANES, LANES), F32),
+                pltpu.VMEM((2, chunk // 2, tile_cols), BF16),
+                pltpu.VMEM((N_CHUNK, 1, chunk), F32),
+                pltpu.VMEM((N_CHUNK, 1, chunk), F32),
+                pltpu.VMEM((N_CHUNK, 1, chunk), F32),
+                pltpu.VMEM((4, 2, n_step, LANES), F32),
+                pltpu.VMEM((m, chunk), F32),
+                dma((3,)),
                 dma((2,)),
+                dma((8,)),
+                dma((2, 5)),
+                dma((2, 2)),
                 dma((2, N_CHUNK)),
                 dma((2, N_CHUNK)),
                 dma((2, 2, N_CHUNK)),
@@ -327,13 +440,9 @@
             ],
             compiler_params=pltpu.CompilerParams(vmem_limit_bytes=67043328, has_side_effects=True),
             name="sweeps",
-        )(edges, x_in, tele, weight, dang, damping)
-
-        pieces = x_out.transpose(1, 3, 0, 2).reshape(2, piece, m)
-        other = lax.ppermute(lax.dynamic_index_in_dim(pieces, 1 - i, 0, False), "row", swap)
-        keeps = lax.axis_index("col") // 2 == i
-        x_final = jnp.where(keeps, lax.dynamic_index_in_dim(pieces, i, 0, False), other)
-        resid = lax.psum(resid[:, :, :half_m].transpose(1, 0, 2).reshape(n_step, m), ("col", "row"))
+        )(adj_tile, x_piece, tele_piece, dang, damping)
+
+        resid = resid[:, :, :half_m].transpose(1, 0, 2).reshape(n_step, m)
         return x_final, resid
 
     vec_spec = P(("col", "row"), None)

time: 1250 us -> 1160 us (0.928)
  other arithmetic: 76.1 us -> 1.3 us
  Pallas kernels: 1110 us -> 1150 us
  local copies, waits for them, and re-layouts: 37.1 us -> 3.74 us
  blocking collectives: 22.2 us -> 0 us
    pallas_call x1, Pallas kernels: 1110 us -> 1150 us  [sweeps(): pl.pallas_call(functools.partial(kernel, n_vert, n_step), out_shape=(jax....]
    reduce_max x1 -> x0, other arithmetic: 36.5 us -> none  [sweeps(): top = jnp.max(adj_tile, axis=0).astype(F32)]
    convert_element_type x3 -> x1, other arithmetic: 33.4 us -> 1.3 us  [sweeps(): dang = dang_piece.astype(F32).reshape(N_SUB, 1, chunk)]
    select_n x4 -> x0, local copies, waits for them, and re-layouts: 22.7 us -> none  [both(): jnp.where(i == 0, jnp.concatenate([own, other]), jnp.concatenate([other,...]
    psum x1 -> x0, blocking collectives: 22.2 us -> none  [sweeps(): lax.psum(resid[:, :, :half_m].transpose(1, 0, 2).reshape(n_step, m), ('co...]
  transfers between devices with their start and end apart: 5 -> 0, of which waited for: 0 -> 0; matrix products, arithmetic and copies ran while one was open for 6% -> 0% of each run, Pallas kernels for 0% -> 0%
where the time goes in v2:
time: 1160 us
  Pallas kernels  1150 us (99%)
    pallas_call x1, Pallas kernels, sweeps(): pl.pallas_call(functools.partial(kernel, n_vert, n_step), out_shape=(jax....  1150 us

profile of v2, /device:TPU:0, one launch (start us, length us, event | category | flops | bytes accessed | tf_op | source)
XLA Modules:
  0.0 1155.7 jit_solution(12769782340032602200)
XLA Ops:
  0.6 1.3 convert_element_type.3
  1.9 1150.0 %sweeps.1 = (f32[2048,128]{1,0:T(8,128)}, f32[2,32,128]{2,1,0:T(8,128)}) custom-call(bf16[8192,4096]{1,0:T(8,128)(2,1)} %a_hbm.1, f32[2048,128]{1,0:T(8,128)} %x_hbm.1, f32[2048,128]{1,0:T(8,128)} %v_hbm.1, f32[4,1,512]{2,1,0:T(1,128)} %bitcast.3, f32[32]{0:T(128)} %damp_ref.1), custom_call_target="tpu_custom_call" | custom-call | tf_op jit(solution)/shard_map/sweeps/pallas_call | solution.py:397
  1152.0 0.8 slice_bitcast_fusion
  1152.8 0.7 reshape.11
  1153.5 2.3 copy.9
  (1 shorter events, 0.0 us)
